TPU v7x, 32 devices: a whole 2x2x4 slice. The times are simulated.
32 devices in a mesh: row: 8 (over y, x, core), col: 4 (over z).
Axes of the slice: x: 2, y: 2, z: 4, core: 2. Of those that a mesh axis runs over, the one named last changes fastest.
Arguments:
- vectors: float32 [32768, 4096], P('row', 'col'), may hold values from -6 to 6
- reflectors: float32 [8, 32768, 128], P('col', 'row'), may hold values from -0.03125 to 0.03125
- triangles: float32 [8, 128, 128], P('col'), may hold values from -0.25 to 1.8, as said below
Outputs:
- transformed: float32 [32768, 4096], P('row', 'col')
Inputs may be any that keep to these rules, and one draw needn't show every extreme that they name: Each triangles[p] is upper triangular with diagonal entries between 0.5 and 1.8.
All inputs are finite; a program needn't handle non-finite values.
Results may differ from a plain program's by a relative error of at most 0.00013.
Values sent between devices are 32-bit elements; how exact they have to be, the bound alone decides.
A program may use at most 128 MiB of HBM per device.

v0:
```python
import jax
import jax.numpy as jnp
from jax import lax
from jax.sharding import PartitionSpec as P


def spread(block, axis, owner):
    block = jnp.where(lax.axis_index(axis) == owner, block, jnp.zeros_like(block))
    return lax.psum(block, axis)


def product_t(left, right):
    return lax.dot_general(
        left,
        right,
        (((0,), (0,)), ((), ())),
        precision=lax.Precision.HIGHEST,
        preferred_element_type=jnp.float32,
    )


def matmul(left, right):
    return jnp.dot(left, right, precision=lax.Precision.HIGHEST, preferred_element_type=jnp.float32)


def shards(vectors, reflectors, triangles):
    per_dev = reflectors.shape[0]
    panels = per_dev * lax.axis_size("col")

    def fetch(panel):
        local = panel % per_dev
        return (
            spread(reflectors[local], "col", panel // per_dev),
            spread(triangles[local], "col", panel // per_dev),
        )

    block = vectors
    for pair in range(panels // 2 - 1, -1, -1):
        basis_a, tri_a = fetch(2 * pair)
        basis_b, tri_b = fetch(2 * pair + 1)
        joined = jnp.concatenate([basis_a, basis_b], axis=1)
        summed, inner = lax.psum((product_t(joined, block), product_t(basis_a, basis_b)), "row")
        width = basis_a.shape[1]
        upper_w = summed[:width]
        lower_w = summed[width:]
        coupling = -matmul(matmul(tri_a, inner), tri_b)
        scaled_a = matmul(tri_a, upper_w) + matmul(coupling, lower_w)
        scaled_b = matmul(tri_b, lower_w)
        block = block - matmul(joined, jnp.concatenate([scaled_a, scaled_b], axis=0))
    return block


def solution(mesh):
    placed = (P("row", "col"), P("col", "row", None), P("col", None, None))
    return jax.shard_map(
        shards, mesh=mesh, in_specs=placed, out_specs=P("row", "col"), check_vma=False
    )
```

profile of v0, /device:TPU:0, one launch (start us, length us, event | category | flops | bytes accessed | tf_op | source)
XLA Modules:
  0.0 1032.6 jit_solution(5668326063415492051)
XLA Ops:
  6.5 1.7 select_bitcast_fusion.9
  8.2 8.2 select_bitcast_fusion
  16.5 582.0 %all-reduce.19.cloned.1.call-done = (f32[4096,128]{1,0:T(8,128)}, f32[4096,128]{1,0:T(8,128)}, f32[128,128]{1,0:T(8,128)}, f32[128,128]{1,0:T(8,128)}, f32[4096,...) async-done(((f32[4096,128]{1,0:T(8,128)}, ...) | async-done | bytes 17301520 | tf_op jit(solution)/shard_map/psum | solution.py:9
  598.5 1.9 constant_dynamic-update-slice_fusion.1
  601.3 4.2 fusion.37
  610.3 2.0 copy-done
  612.4 30.1 %fusion.36 = f32[256,1024]{1,0:T(8,128)} fusion(f32[4096,256]{1,0:T(8,128)S(1)} %constant_dynamic-update-slice_fusion, f32[4096,1024]{1,0:T(8,128)} %param.3), kind=kOutput, calls=%fused_computation.72 | convolution fusion | flops 12884901888 | bytes 22020096 | tf_op jit(solution)/shard_map/dot_general | solution.py:13
  642.8 5.7 fusion.40
  650.0 48.5 %all-reduce.17.cloned.1.call-done = (f32[256,1024]{1,0:T(8,128)}, f32[128,128]{1,0:T(8,128)}) async-done(((f32[256,1024]{1,0:T(8,128)}, f32[128,128]{1,0:T(8,128)}), (f32[256,1024]{1,0:T(8,128)}, f32[128,128]{1,0:T(8,128)})) %all-reduce.17.cloned.1.call-update) | async-done | bytes 1114128 | tf_op jit(solution)/shard_map/psum | solution.py:42
  699.7 1.7 fusion.18
  703.3 1.6 convolution_add_fusion.3
  704.9 18.7 %convolution_subtract_fusion.3 = f32[4096,1024]{1,0:T(8,128)} fusion(f32[4096,1024]{1,0:T(8,128)} %param.3, f32[4096,256]{1,0:T(8,128)S(1)} %copy-done.1, f32[128,1024]{1,0:T(8,128)S(1)} %fusion.29, f32[128,1024]{1,0:T(8,128)S(1)} %convolution_add_fusion.3), kind=kOutput, calls=%fused_computation.3 | convolution fusion | flops 12889358336 | bytes 38797312 | tf_op jit(solution)/shard_map/dot_general | solution.py:23
  723.7 18.1 %fusion.39 = f32[256,1024]{1,0:T(8,128)} fusion(f32[4096,256]{1,0:T(8,128)} %constant_dynamic-update-slice_fusion.2, f32[4096,1024]{1,0:T(8,128)} %convolution_subtract_fusion.3), kind=kOutput, calls=%fused_computation.75 | convolution fusion | flops 12884901888 | bytes 22020096 | tf_op jit(solution)/shard_map/dot_general | solution.py:13
  742.4 5.7 fusion.43
  749.6 48.8 %all-reduce.15.cloned.1.call-done = (f32[256,1024]{1,0:T(8,128)}, f32[128,128]{1,0:T(8,128)}) async-done(((f32[256,1024]{1,0:T(8,128)}, f32[128,128]{1,0:T(8,128)}), (f32[256,1024]{1,0:T(8,128)}, f32[128,128]{1,0:T(8,128)})) %all-reduce.15.cloned.1.call-update) | async-done | bytes 1114128 | tf_op jit(solution)/shard_map/psum | solution.py:42
  802.9 1.6 convolution_add_fusion.2
  804.5 19.8 %convolution_subtract_fusion.2 = f32[4096,1024]{1,0:T(8,128)} fusion(f32[4096,1024]{1,0:T(8,128)} %convolution_subtract_fusion.3, f32[4096,256]{1,0:T(8,128)} %constant_dynamic-update-slice_fusion.2, f32[128,1024]{1,0:T(8,128)S(1)} %fusion.26, f32[128,1024]{1,0:T(8,128)S(1)} %convolution_add_fusion.2), kind=kOutput, calls=%fused_computation.2 | convolution fusion | flops 12889358336 | bytes 38797312 | tf_op jit(solution)/shard_map/dot_general | solution.py:23
  824.3 18.2 %fusion.42 = f32[256,1024]{1,0:T(8,128)} fusion(f32[4096,256]{1,0:T(8,128)} %constant_dynamic-update-slice_fusion.4, f32[4096,1024]{1,0:T(8,128)} %convolution_subtract_fusion.2), kind=kOutput, calls=%fused_computation.78 | convolution fusion | flops 12884901888 | bytes 22020096 | tf_op jit(solution)/shard_map/dot_general | solution.py:13
  842.7 5.7 fusion.46
  850.0 49.0 %all-reduce.13.cloned.1.call-done = (f32[256,1024]{1,0:T(8,128)}, f32[128,128]{1,0:T(8,128)}) async-done(((f32[256,1024]{1,0:T(8,128)}, f32[128,128]{1,0:T(8,128)}), (f32[256,1024]{1,0:T(8,128)}, f32[128,128]{1,0:T(8,128)})) %all-reduce.13.cloned.1.call-update) | async-done | bytes 1114128 | tf_op jit(solution)/shard_map/psum | solution.py:42
  905.1 19.8 %convolution_subtract_fusion.1 = f32[4096,1024]{1,0:T(8,128)} fusion(f32[4096,1024]{1,0:T(8,128)} %convolution_subtract_fusion.2, f32[4096,256]{1,0:T(8,128)} %constant_dynamic-update-slice_fusion.4, f32[128,1024]{1,0:T(8,128)S(1)} %fusion.23, f32[128,1024]{1,0:T(8,128)S(1)} %convolution_add_fusion.1), kind=kOutput, calls=%fused_computation.1 | convolution fusion | flops 12889358336 | bytes 38797312 | tf_op jit(solution)/shard_map/dot_general | solution.py:23
  925.0 18.0 %fusion.45 = f32[256,1024]{1,0:T(8,128)} fusion(f32[4096,256]{1,0:T(8,128)} %constant_dynamic-update-slice_fusion.6, f32[4096,1024]{1,0:T(8,128)} %convolution_subtract_fusion.1), kind=kOutput, calls=%fused_computation.81 | convolution fusion | flops 12884901888 | bytes 22020096 | tf_op jit(solution)/shard_map/dot_general | solution.py:13
  943.0 56.5 %all-reduce.11.cloned.1.call-done = (f32[256,1024]{1,0:T(8,128)}, f32[128,128]{1,0:T(8,128)}) async-done(((f32[256,1024]{1,0:T(8,128)}, f32[128,128]{1,0:T(8,128)}), (f32[256,1024]{1,0:T(8,128)}, f32[128,128]{1,0:T(8,128)})) %all-reduce.11.cloned.1.call-update) | async-done | bytes 1114128 | tf_op jit(solution)/shard_map/psum | solution.py:42
  1005.7 19.9 %convolution_subtract_fusion = f32[4096,1024]{1,0:T(8,128)} fusion(f32[4096,1024]{1,0:T(8,128)} %convolution_subtract_fusion.1, f32[4096,256]{1,0:T(8,128)} %constant_dynamic-update-slice_fusion.6, f32[128,1024]{1,0:T(8,128)S(1)} %fusion.20, f32[128,1024]{1,0:T(8,128)S(1)} %convolution_add_fusion), kind=kOutput, calls=%fused_computation | convolution fusion | flops 12889358336 | bytes 38797312 | tf_op jit(solution)/shard_map/dot_general | solution.py:23
  (69 shorter events, 31.1 us)
Async XLA Ops:
  6.5 591.9 %all-reduce.19.cloned.1.call-start = ((), (), s32[]{:S(2)}) async-start(), calls=%async_computation.4 | async-start | bytes 34603008 | tf_op jit(solution)/shard_map/psum | solution.py:9
  16.4 682.1 %all-reduce.17.cloned.1.call-start = ((), (), s32[]{:S(2)}) async-start(), calls=%async_computation.3 | async-start | bytes 2228224 | tf_op jit(solution)/shard_map/psum | solution.py:42
  598.5 2.2 copy-start.8
  598.5 2.9 copy-start.9
  598.5 7.1 copy-start.3
  601.3 5.8 copy-start.5
  605.6 3.1 copy-start.7
  610.3 2.0 copy-start
  612.4 30.4 %copy-start.6 = (f32[4096,128]{1,0:T(8,128)S(1)}, f32[4096,128]{1,0:T(8,128)}, u32[]{:S(2)}) copy-start(f32[4096,128]{1,0:T(8,128)} %get-tuple-element.18) | copy-start | bytes 6291460
  642.5 155.8 %all-reduce.15.cloned.1.call-start = ((), (), s32[]{:S(2)}) async-start(), calls=%async_computation.2 | async-start | bytes 2228224 | tf_op jit(solution)/shard_map/psum | solution.py:42
  642.8 55.7 %copy-start.17 = (f32[128,128]{1,0:T(8,128)S(1)}, f32[128,128]{1,0:T(8,128)}, u32[]{:S(2)}) copy-start(f32[128,128]{1,0:T(8,128)} %get-tuple-element.16) | copy-start | bytes 196612
  642.8 58.6 %copy-start.16 = (f32[128,128]{1,0:T(8,128)S(1)}, f32[128,128]{1,0:T(8,128)}, u32[]{:S(2)}) copy-start(f32[128,128]{1,0:T(8,128)} %get-tuple-element.15) | copy-start | bytes 196612
  698.5 6.4 copy-start.1
  723.7 18.7 %copy-start.4 = (f32[4096,128]{1,0:T(8,128)S(1)}, f32[4096,128]{1,0:T(8,128)}, u32[]{:S(2)}) copy-start(f32[4096,128]{1,0:T(8,128)} %get-tuple-element.22) | copy-start | bytes 6291460
  741.8 157.1 %all-reduce.13.cloned.1.call-start = ((), (), s32[]{:S(2)}) async-start(), calls=%async_computation.1 | async-start | bytes 2228224 | tf_op jit(solution)/shard_map/psum | solution.py:42
  742.4 56.0 %copy-start.15 = (f32[128,128]{1,0:T(8,128)S(1)}, f32[128,128]{1,0:T(8,128)}, u32[]{:S(2)}) copy-start(f32[128,128]{1,0:T(8,128)} %get-tuple-element.20) | copy-start | bytes 196612
  742.4 58.7 %copy-start.14 = (f32[128,128]{1,0:T(8,128)S(1)}, f32[128,128]{1,0:T(8,128)}, u32[]{:S(2)}) copy-start(f32[128,128]{1,0:T(8,128)} %get-tuple-element.19) | copy-start | bytes 196612
  824.3 18.4 %copy-start.2 = (f32[4096,128]{1,0:T(8,128)S(1)}, f32[4096,128]{1,0:T(8,128)}, u32[]{:S(2)}) copy-start(f32[4096,128]{1,0:T(8,128)} %get-tuple-element.26) | copy-start | bytes 6291460
  842.5 157.1 %all-reduce.11.cloned.1.call-start = ((), (), s32[]{:S(2)}) async-start(), calls=%async_computation | async-start | bytes 2228224 | tf_op jit(solution)/shard_map/psum | solution.py:42
  842.7 56.3 %copy-start.13 = (f32[128,128]{1,0:T(8,128)S(1)}, f32[128,128]{1,0:T(8,128)}, u32[]{:S(2)}) copy-start(f32[128,128]{1,0:T(8,128)} %get-tuple-element.24) | copy-start | bytes 196612
  842.7 58.9 %copy-start.12 = (f32[128,128]{1,0:T(8,128)S(1)}, f32[128,128]{1,0:T(8,128)}, u32[]{:S(2)}) copy-start(f32[128,128]{1,0:T(8,128)} %get-tuple-element.23) | copy-start | bytes 196612
  925.0 74.6 %copy-start.11 = (f32[128,128]{1,0:T(8,128)S(1)}, f32[128,128]{1,0:T(8,128)}, u32[]{:S(2)}) copy-start(f32[128,128]{1,0:T(8,128)} %get-tuple-element.28) | copy-start | bytes 196612
  925.0 77.3 %copy-start.10 = (f32[128,128]{1,0:T(8,128)S(1)}, f32[128,128]{1,0:T(8,128)}, u32[]{:S(2)}) copy-start(f32[128,128]{1,0:T(8,128)} %get-tuple-element.27) | copy-start | bytes 196612
Sparse Core Ops, SparseCore 0:
  16.6 581.8 all-reduce.18
  642.6 55.8 all-reduce.16
  742.0 56.3 all-reduce.14
  842.6 56.3 all-reduce.12
  943.2 56.3 all-reduce.10
where the time goes:
time: 1040 us; the launch traced here: 1030 us
  waiting for transfers between devices  785 us (75%)
  matrix products  209 us (20%)
  local copies, waits for them, and re-layouts  14.2 us (1%)
  between operations  14 us (1%)
    psum x1, waiting for transfers between devices, spread(): return lax.psum(block, axis)  582 us
    psum x4, waiting for transfers between devices, shards(): lax.psum((product_t(joined, block), product_t(basis_a, basis_b)), 'row')  203 us
    dot_general x8, matrix products, product_t(): lax.dot_general(left, right, (((0,), (0,)), ((), ())), precision=lax.Prec...  106 us
    dot_general x24, matrix products, matmul(): jnp.dot(left, right, precision=lax.Precision.HIGHEST, preferred_element_t...  103 us
  transfers between devices with their start and end apart: 5, of which 5 were waited for; matrix products, arithmetic and copies ran while one was open for 2% of the time, Pallas kernels for 0%

commit v1 on v0

v1 whole, which is shorter than its diff:
```python
import jax
import jax.numpy as jnp
from jax import lax
from jax.sharding import PartitionSpec as P

FULL = lax.Precision.HIGHEST
THREE = lax.Precision.HIGH


def product_t(left, right, precision=THREE):
    return lax.dot_general(
        left,
        right,
        (((0,), (0,)), ((), ())),
        precision=precision,
        preferred_element_type=jnp.float32,
    )


def matmul(left, right, precision=THREE):
    return jnp.dot(left, right, precision=precision, preferred_element_type=jnp.float32)


def merge(tri_a, inner, tri_b):
    coupling = -matmul(matmul(tri_a, inner, FULL), tri_b, FULL)
    zero = jnp.zeros((tri_b.shape[0], tri_a.shape[1]), jnp.float32)
    return jnp.concatenate(
        [
            jnp.concatenate([tri_a, coupling], axis=1),
            jnp.concatenate([zero, tri_b], axis=1),
        ],
        axis=0,
    )


def after(value, earlier):
    return value + 0.0 * sum(array[0, 0] for array in earlier)


def ring_gather(panels, n):
    up = [(i, (i + 1) % n) for i in range(n)]
    down = [(i, (i - 1) % n) for i in range(n)]
    count = len(panels)
    near = {0: list(panels)}
    lower, upper = list(panels), list(panels)
    for step in range(1, (n - 1) // 2 + 1):
        lower = [lax.ppermute(lower[i], "col", up) for i in range(count)]
        upper = [lax.ppermute(upper[i], "col", down) for i in reversed(range(count))][::-1]
        near[n - step] = lower
        near[step] = upper
    if n % 2 == 0:
        half = (count + 1) // 2
        near[n // 2] = [lax.ppermute(lower[i], "col", up) for i in range(half)] + [
            lax.ppermute(upper[i], "col", down) for i in range(half, count)
        ]
    return near


def shards(vectors, reflectors, triangles):
    per_dev, _, nb = reflectors.shape
    n = lax.axis_size("col")
    rows = lax.axis_size("row")
    me = lax.axis_index("col")
    width = per_dev * nb

    near = ring_gather([reflectors[i] for i in range(per_dev)], n)
    basis = {r: jnp.concatenate(near[r], axis=1) for r in range(n)}

    summed = {}
    summed[0], inner = lax.psum((product_t(basis[0], vectors), product_t(basis[0], basis[0], FULL)), "row")
    tri = triangles[0]
    for i in range(1, per_dev):
        tri = merge(tri, inner[: i * nb, i * nb : (i + 1) * nb], triangles[i])

    last = n // 2
    pairs = []
    for d in range(1, n // 2 + 1):
        low, high = (-(d // 2)) % n, (d - d // 2) % n
        pairs.append(product_t(basis[low], basis[high], FULL))
    share = width // rows
    mine = [lax.dynamic_slice_in_dim(tri, lax.axis_index("row") * share, share, 0)]
    if pairs:
        split = lax.psum_scatter(jnp.stack(pairs), "row", scatter_dimension=1, tiled=True)
        mine += [split[i] for i in range(len(pairs))]
    shared = lax.all_gather(jnp.stack(mine), ("col", "row"), axis=0)
    shared = shared.reshape(n, rows, len(mine), share, width)
    shared = shared.transpose(0, 2, 1, 3, 4).reshape(n, len(mine), width, width)

    def inner_of(i, j):
        ahead = j - i
        d = min(ahead, n - ahead)
        if ahead == d:
            return shared[(i + d // 2) % n, d]
        return shared[(j + d // 2) % n, d].T

    tris = [(i, i + 1, shared[i, 0]) for i in range(n)]
    while len(tris) > 1:
        merged = []
        for a, b in zip(tris[::2], tris[1::2]):
            inner_ab = jnp.concatenate(
                [jnp.concatenate([inner_of(i, j) for j in range(b[0], b[1])], axis=1) for i in range(a[0], a[1])],
                axis=0,
            )
            merged.append((a[0], b[1], merge(a[2], inner_ab, b[2])))
        if len(tris) % 2:
            merged.append(tris[-1])
        tris = merged
    whole = tris[0][2].reshape(n, width, n, width)
    whole = lax.dynamic_slice_in_dim(jnp.concatenate([whole, whole], axis=0), me, n, 0)
    whole = whole.transpose(2, 0, 1, 3)
    whole = lax.dynamic_slice_in_dim(jnp.concatenate([whole, whole], axis=0), me, n, 0)
    columns = [whole[r].reshape(n * width, width) for r in range(n)]

    early = [r for r in range(1, n) if r != last]
    if early:
        joined = product_t(jnp.concatenate([basis[r] for r in early], axis=1), vectors)
        joined = lax.psum(after(joined, [summed[0], inner] + pairs), "row")
        for at, r in enumerate(early):
            summed[r] = joined[at * width : (at + 1) * width]
    order = [0] + early
    scaled = matmul(
        jnp.concatenate([columns[r] for r in order], axis=1),
        jnp.concatenate([summed[r] for r in order], axis=0),
    )
    if n > 1:
        done = [summed[early[-1]] if early else summed[0]]
        summed[last] = lax.psum(after(product_t(basis[last], vectors), done), "row")
        scaled = scaled + matmul(columns[last], summed[last])
    return vectors - matmul(jnp.concatenate([basis[r] for r in range(n)], axis=1), scaled)


def solution(mesh):
    placed = (P("row", "col"), P("col", "row", None), P("col", None, None))
    return jax.shard_map(
        shards, mesh=mesh, in_specs=placed, out_specs=P("row", "col"), check_vma=False
    )
```

time: 1040 us -> 495 us (0.48)
  waiting for transfers between devices: 785 us -> 265 us
  matrix products: 209 us -> 126 us
  local copies, waits for them, and re-layouts: 14.2 us -> 51.2 us
  starting transfers between devices: 1.06 us -> 13.3 us
    psum x5 -> x3, waiting for transfers between devices: 785 us -> 131 us  [the longest x1 59.5 us: shards(): joined = lax.psum(after(joined, [summed[0], inner] + pairs), 'row')]
    ppermute x0 -> x6, waiting for transfers between devices: none -> 107 us  [the longest x3 74.6 us: ring_gather(): lax.ppermute(upper[i], 'col', down)]
    dot_general x32 -> x17, matrix products: 209 us -> 126 us  [the longest x6 71 us: product_t(): lax.dot_general(left, right, (((0,), (0,)), ((), ())), precision=precisio...]
    all_gather x0 -> x1, waiting for transfers between devices: none -> 16.2 us  [shards(): shared = lax.all_gather(jnp.stack(mine), ('col', 'row'), axis=0)]
    unnamed x40 -> x31, local copies, waits for them, and re-layouts: 9.51 us -> 25.4 us
    ppermute x0 -> x6, starting transfers between devices: none -> 12.9 us  [the longest x3 11.4 us: ring_gather(): lax.ppermute(upper[i], 'col', down)]
  transfers between devices with their start and end apart: 5 -> 11, of which waited for: 5 -> 8; matrix products, arithmetic and copies ran while one was open for 2% -> 27% of each run, Pallas kernels for 0% -> 0%
where the time goes in v1:
time: 495 us; the launch traced here: 486 us
  waiting for transfers between devices  265 us (54%)
  matrix products  126 us (25%)
  local copies, waits for them, and re-layouts  51.2 us (10%)
  between operations  17 us (3%)
  other arithmetic  14.1 us (3%)
  starting transfers between devices  13.3 us (3%)
    ppermute x3, waiting for transfers between devices, ring_gather(): lax.ppermute(upper[i], 'col', down)  74.6 us
    dot_general x6, matrix products, product_t(): lax.dot_general(left, right, (((0,), (0,)), ((), ())), precision=precisio...  71 us
    psum x1, waiting for transfers between devices, shards(): joined = lax.psum(after(joined, [summed[0], inner] + pairs), 'row')  59.5 us
    dot_general x11, matrix products, matmul(): jnp.dot(left, right, precision=precision, preferred_element_type=jnp.floa...  54.5 us
    psum x1, waiting for transfers between devices, shards(): lax.psum((product_t(basis[0], vectors), product_t(basis[0], basis[0], FUL...  54.5 us
    ppermute x2, waiting for transfers between devices, ring_gather(): lower = [lax.ppermute(lower[i], 'col', up) for i in range(count)]  32.8 us
    unnamed x31, local copies, waits for them, and re-layouts  25.4 us
    psum x1, waiting for transfers between devices, shards(): summed[last] = lax.psum(after(product_t(basis[last], vectors), done), 'row')  17 us
  transfers between devices with their start and end apart: 11, of which 8 were waited for; matrix products, arithmetic and copies ran while one was open for 27% of the time, Pallas kernels for 0%

profile of v1, /device:TPU:0, one launch (start us, length us, event | category | flops | bytes accessed | tf_op | source)
XLA Modules:
  0.0 486.1 jit_solution(1574006051985618780)
XLA Ops:
  6.5 3.8 slice_bitcast_fusion
  10.3 5.1 %collective-permute-start = (f32[4096,128]{1,0:T(8,128)}, f32[4096,128]{1,0:T(8,128)}, u32[]{:S(2)}, u32[]{:S(2)}) collective-permute-start(f32[4096,128]{1,0:T(8,128)} %get-tuple-element.12), channel_id=1, source_target_pairs={{0,3},{1,0},{2,1},{3,2},{4,7},{5,4},{6,5},{7,6},{8,11},{9,8},{10,9... | collective-permute-start | bytes 6291464 | tf_op jit(solution)/shard_map/ppermute | solution.py:48
  15.4 3.8 collective-permute-start.1
  19.3 11.7 %fusion.29 = f32[256,1024]{1,0:T(8,128)} fusion(f32[4096,1024]{1,0:T(8,128)} %param.3, f32[4096,128]{1,0:T(8,128)S(1)} %get-tuple-element.11, f32[4096,128]{1,0:T(8,128)} %get-tuple-element.12), kind=kOutput, calls=%fused_computation.37 | convolution fusion | flops 6443499520 | bytes 22020096 | tf_op jit(solution)/shard_map/dot_general | solution.py:11
  31.0 9.7 %fusion.31 = f32[256,256]{1,0:T(8,128)} fusion(f32[4096,128]{1,0:T(8,128)S(1)} %get-tuple-element.11, f32[4096,128]{1,0:T(8,128)} %get-tuple-element.12), kind=kOutput, calls=%fused_computation.39 | convolution fusion | flops 3222274048 | bytes 4456448 | tf_op jit(solution)/shard_map/dot_general | solution.py:11
  41.0 3.3 constant_dynamic-update-slice_fusion.7
  45.8 54.5 %all-reduce.13.cloned.1.call-done = (f32[256,256]{1,0:T(8,128)}, f32[256,1024]{1,0:T(8,128)}) async-done(((f32[256,256]{1,0:T(8,128)}, f32[256,1024]{1,0:T(8,128)}), (f32[256,256]{1,0:T(8,128)}, f32[256,1024]{1,0:T(8,128)})) %all-reduce.13.cloned.1.call-update) | async-done | bytes 1310736 | tf_op jit(solution)/shard_map/psum | solution.py:70
  104.1 3.2 constant_dynamic-update-slice_fusion.9
  107.3 44.3 %collective-permute-done.1 = f32[4096,128]{1,0:T(8,128)} collective-permute-done((f32[4096,128]{1,0:T(8,128)S(1)}, f32[4096,128]{1,0:T(8,128)}, u32[]{:S(2)}, u32[]{:S(2)}) %collective-permute-start.1) | collective-permute-done | bytes 2097184 | tf_op jit(solution)/shard_map/ppermute | solution.py:48
  154.8 8.3 %fusion.30 = f32[256,256]{1,0:T(8,128)S(1)} fusion(f32[4096,256]{1,0:T(8,128)S(1)} %get-tuple-element.21, f32[4096,128]{1,0:T(8,128)S(1)} %get-tuple-element.11, f32[4096,128]{1,0:T(8,128)} %get-tuple-element.12), kind=kOutput, calls=%fused_computation.38 | convolution fusion | flops 3222274048 | bytes 8650752 | tf_op jit(solution)/shard_map/dot_general | solution.py:11
  163.6 32.8 %collective-permute-done.5 = f32[4096,128]{1,0:T(8,128)} collective-permute-done((f32[4096,128]{1,0:T(8,128)S(1)}, f32[4096,128]{1,0:T(8,128)}, u32[]{:S(2)}, u32[]{:S(2)}) %collective-permute-start.5) | collective-permute-done | bytes 2097184 | tf_op jit(solution)/shard_map/ppermute | solution.py:47
  196.4 9.4 %fusion.11 = f32[256,256]{1,0:T(8,128)S(1)} fusion(f32[4096,256]{1,0:T(8,128)S(1)} %get-tuple-element.21, f32[4096,128]{1,0:T(8,128)} %collective-permute-done.5, f32[4096,128]{1,0:T(8,128)} %collective-permute-done.2), kind=kOutput, calls=%fused_computation.19 | convolution fusion | flops 3222274048 | bytes 8650752 | tf_op jit(solution)/shard_map/dot_general | solution.py:11
  208.4 20.0 %fusion.32 = f32[512,1024]{1,0:T(8,128)} fusion(f32[4096,1024]{1,0:T(8,128)} %param.3, f32[4096,128]{1,0:T(8,128)} %collective-permute-done.5, f32[4096,128]{1,0:T(8,128)} %collective-permute-done.2, f32[4096,128]{1,0:T(8,128)} %collective-permute-done.1, f32[4096,128]{1,0:T(8,128)} %collective-permute-done, f32[]{:T(128)} %bitcast.22), kind=kOutput, calls=%fused_computation.42 | convolution fusion | flops 12891717632 | bytes 27262980 | tf_op jit(solution)/shard_map/dot_general | solution.py:11
  230.4 10.3 %reduce-scatter.2.cloned.1.call-done = f32[2,32,256]{2,1,0:T(8,128)} async-done(((f32[2,256,256]{2,1,0:T(8,128)}), f32[2,32,256]{2,1,0:T(8,128)}) %reduce-scatter.2.cloned.1.call-update) | async-done | bytes 65552 | tf_op jit(solution)/shard_map/reduce_scatter | solution.py:83
  246.4 59.5 %all-reduce.9.cloned.1.call-done = f32[512,1024]{1,0:T(8,128)} async-done(((f32[512,1024]{1,0:T(8,128)}), f32[512,1024]{1,0:T(8,128)}) %all-reduce.9.cloned.1.call-update) | async-done | bytes 2097168 | tf_op jit(solution)/shard_map/psum | solution.py:117
  307.7 30.3 %collective-permute-done.4 = f32[4096,128]{1,0:T(8,128)} collective-permute-done((f32[4096,128]{1,0:T(8,128)}, f32[4096,128]{1,0:T(8,128)}, u32[]{:S(2)}, u32[]{:S(2)}) %collective-permute-start.4) | collective-permute-done | bytes 2097184 | tf_op jit(solution)/shard_map/ppermute | solution.py:54
  338.0 11.8 %fusion.35 = f32[256,1024]{1,0:T(8,128)} fusion(f32[4096,1024]{1,0:T(8,128)} %param.3, f32[4096,128]{1,0:T(8,128)} %collective-permute-done.4, f32[4096,128]{1,0:T(8,128)S(1)} %collective-permute-done.3, f32[]{:T(128)} %bitcast.23), kind=kOutput, calls=%fused_computation.44 | convolution fusion | flops 6443761664 | bytes 22020100 | tf_op jit(solution)/shard_map/dot_general | solution.py:11
  360.6 16.2 %all-gather.3.cloned.1.call-done = f32[96,32,256]{2,1,0:T(8,128)} async-done(((f32[3,32,256]{2,1,0:T(8,128)}), f32[96,32,256]{2,1,0:T(8,128)}) %all-gather.3.cloned.1.call-update) | async-done | bytes 3145744 | tf_op jit(solution)/shard_map/all_gather | solution.py:85
  402.0 5.8 %reshape.18 = f32[4,256,4,256]{1,0,3,2:T(4,128)} reshape(f32[1024,1024]{0,1:T(8,128)} %select_maximum_fusion) | data formatting | bytes 8388608 | tf_op jit(solution)/shard_map/reshape | solution.py:108
  407.8 6.5 %fusion.10 = f32[4,4,256,256]{2,1,3,0:T(4,128)S(1)} fusion(s32[]{:T(128)S(6)} %select_n.8, f32[4,256,4,256]{1,0,3,2:T(4,128)} %reshape.18), kind=kLoop, calls=%fused_computation.15 | loop fusion | flops 1048576 | bytes 8388612 | tf_op jit(solution)/shard_map/transpose | solution.py:110
  418.3 17.0 %all-reduce.11.cloned.1.call-done = f32[256,1024]{1,0:T(8,128)} async-done(((f32[256,1024]{1,0:T(8,128)}), f32[256,1024]{1,0:T(8,128)}) %all-reduce.11.cloned.1.call-update) | async-done | bytes 1048592 | tf_op jit(solution)/shard_map/psum | solution.py:127
  435.3 3.2 fusion.80
  438.6 6.7 %fusion.20 = f32[1024,1024]{1,0:T(8,128)} fusion(f32[1024,256]{0,1:T(8,128)S(1)} %bitcast.111, f32[1024,256]{0,1:T(8,128)S(1)} %bitcast.110, f32[1024,256]{0,1:T(8,128)S(1)} %bitcast.109, f32[512,1024]{1,0:T(8,128)S(1)} %copy-done.5, f32[256,1024]{1,0:T(8,128)S(1)} %copy-done.6), kind=kOutput, calls=%fused_computation.28 | convolution fusion | flops 4834197504 | bytes 10485760 | tf_op jit(solution)/shard_map/dot_general | solution.py:21
  445.3 33.8 %convolution_subtract_fusion = f32[4096,1024]{1,0:T(8,128)} fusion(f32[4096,1024]{1,0:T(8,128)} %param.3, f32[4096,1024]{1,0:T(8,128)} %constant_dynamic-update-slice_fusion, f32[1024,1024]{1,0:T(8,128)} %fusion.20, f32[1024,1024]{1,0:T(8,128)S(1)} %fusion.80), kind=kOutput, calls=%fused_computation.12 | convolution fusion | flops 25775046656 | bytes 58720256 | tf_op jit(solution)/shard_map/dot_general | solution.py:21
  (73 shorter events, 58.0 us)
Async XLA Ops:
  6.5 93.7 %all-reduce.13.cloned.1.call-start = ((), (), s32[]{:S(2)}) async-start(), calls=%async_computation.5 | async-start | bytes 2621440 | tf_op jit(solution)/shard_map/psum | solution.py:70
  10.3 93.7 %collective-permute-start = (f32[4096,128]{1,0:T(8,128)}, f32[4096,128]{1,0:T(8,128)}, u32[]{:S(2)}, u32[]{:S(2)}) collective-permute-start(f32[4096,128]{1,0:T(8,128)} %get-tuple-element.12), channel_id=1, source_target_pairs={{0,3},{1,0},{2,1},{3,2},{4,7},{5,4},{6,5},{7,6},{8,11},{9,8},{10,9... | collective-permute-start | bytes 6291464 | tf_op jit(solution)/shard_map/ppermute | solution.py:48
  15.4 148.2 %collective-permute-start.2 = (f32[4096,128]{1,0:T(8,128)}, f32[4096,128]{1,0:T(8,128)}, u32[]{:S(2)}, u32[]{:S(2)}) collective-permute-start(f32[4096,128]{1,0:T(8,128)} %get-tuple-element.12), channel_id=1, source_target_pairs={{0,1},{1,2},{2,3},{3,0},{4,5},{5,6},{6,7},{7,4},{8,9},{9,10},{10,1... | collective-permute-start | bytes 6291464 | tf_op jit(solution)/shard_map/ppermute | solution.py:47
  15.4 136.2 %collective-permute-start.1 = (f32[4096,128]{1,0:T(8,128)S(1)}, f32[4096,128]{1,0:T(8,128)}, u32[]{:S(2)}, u32[]{:S(2)}) collective-permute-start(f32[4096,128]{1,0:T(8,128)S(1)} %get-tuple-element.11), channel_id=1, source_target_pairs={{0,3},{1,0},{2,1},{3,2},{4,7},{5,4},{6,5},{7,6},{8,11},{9,8},{10,9... | collective-permute-start | bytes 6291464 | tf_op jit(solution)/shard_map/ppermute | solution.py:48
  19.3 177.2 %collective-permute-start.5 = (f32[4096,128]{1,0:T(8,128)S(1)}, f32[4096,128]{1,0:T(8,128)}, u32[]{:S(2)}, u32[]{:S(2)}) collective-permute-start(f32[4096,128]{1,0:T(8,128)S(1)} %get-tuple-element.11), channel_id=1, source_target_pairs={{0,1},{1,2},{2,3},{3,0},{4,5},{5,6},{6,7},{7,4},{8,9},{9,10},{10,1... | collective-permute-start | bytes 6291464 | tf_op jit(solution)/shard_map/ppermute | solution.py:47
  40.7 200.1 %reduce-scatter.2.cloned.1.call-start = ((), (), s32[]{:S(2)}) async-start(), calls=%async_computation.1 | async-start | bytes 589824 | tf_op jit(solution)/shard_map/reduce_scatter | solution.py:83
  41.0 3.3 copy-start
  207.2 98.7 %all-reduce.9.cloned.1.call-start = ((), (), s32[]{:S(2)}) async-start(), calls=%async_computation.2 | async-start | bytes 4194304 | tf_op jit(solution)/shard_map/psum | solution.py:117
  208.4 20.1 %copy-start.4 = (f32[2,128,128]{2,1,0:T(8,128)S(1)}, f32[2,128,128]{2,1,0:T(8,128)}, u32[]{:S(2)}) copy-start(f32[2,128,128]{2,1,0:T(8,128)} %param.5) | copy-start | bytes 393220
  228.5 148.3 %all-gather.3.cloned.1.call-start = ((), (), s32[]{:S(2)}) async-start(), calls=%async_computation.4 | async-start | bytes 3244032 | tf_op jit(solution)/shard_map/all_gather | solution.py:85
  242.3 193.0 %all-reduce.11.cloned.1.call-start = ((), (), s32[]{:S(2)}) async-start(), calls=%async_computation.3 | async-start | bytes 2097152 | tf_op jit(solution)/shard_map/psum | solution.py:127
  242.3 65.3 %collective-permute-start.3 = (f32[4096,128]{1,0:T(8,128)}, f32[4096,128]{1,0:T(8,128)S(1)}, u32[]{:S(2)}, u32[]{:S(2)}) collective-permute-start(f32[4096,128]{1,0:T(8,128)} %collective-permute-done.2), channel_id=1, source_target_pairs={{0,1},{1,2},{2,3},{3,0},{4,5},{5,6},{6,7},{7,4},{8,9},{9,10},{10,1... | collective-permute-start | bytes 6291464 | tf_op jit(solution)/shard_map/ppermute | solution.py:53
  243.9 94.1 %collective-permute-start.4 = (f32[4096,128]{1,0:T(8,128)}, f32[4096,128]{1,0:T(8,128)}, u32[]{:S(2)}, u32[]{:S(2)}) collective-permute-start(f32[4096,128]{1,0:T(8,128)} %collective-permute-done.1), channel_id=1, source_target_pairs={{0,3},{1,0},{2,1},{3,2},{4,7},{5,4},{6,5},{7,6},{8,11},{9,8},{10,9... | collective-permute-start | bytes 6291464 | tf_op jit(solution)/shard_map/ppermute | solution.py:54
  390.0 7.5 %copy-start.1 = (f32[256,256]{0,1:T(8,128)S(1)}, f32[256,256]{0,1:T(8,128)}, u32[]{:S(2)}) copy-start(f32[256,256]{0,1:T(8,128)} %convolution_negate_fusion.1) | copy-start | bytes 786436
  393.3 6.2 %copy-start.2 = (f32[1,1,256,256]{2,3,1,0:T(8,128)S(1)}, f32[1,1,256,256]{2,3,1,0:T(8,128)}, u32[]{:S(2)}) copy-start(f32[1,1,256,256]{2,3,1,0:T(8,128)} %copy.36) | copy-start | bytes 786436
  435.3 3.2 copy-start.3
  435.3 3.3 copy-start.5
  435.3 3.3 copy-start.6
Sparse Core Ops, SparseCore 0:
  40.8 59.3 all-reduce.12
  207.3 33.4 reduce-scatter.1
  244.0 61.7 all-reduce.8
  308.5 68.2 all-gather.2
  379.8 55.4 all-reduce.10
